TPU v7x, 32 devices: a whole 2x2x4 slice. The times are simulated.
32 devices in a mesh: groups: 2 (over y), seq: 4 (over z), section: 2 (over x), mp: 2 (over core).
Axes of the slice: x: 2, y: 2, z: 4, core: 2. Of those that a mesh axis runs over, the one named last changes fastest.
Arguments:
- light_queries: bfloat16 [2048, 8192], P(('groups', 'seq'), ('section', 'mp')), parts along dimension 0, may hold values from -6 to 6
- light_keys: bfloat16 [2048, 8192], P(('groups', 'seq'), ('section', 'mp')), parts along dimension 0, may hold values from -6 to 6
- light_values: bfloat16 [2048, 8192], P(('groups', 'seq'), ('section', 'mp')), parts along dimension 0, may hold values from -6 to 6
- decay_log: float32 [2048, 64], P(('groups', 'seq'), ('section', 'mp')), parts along dimension 0, may hold values from -1 to 0
- norm_gain: float32 [8192], P(('section', 'mp')), may hold values from 0.25 to 1.75
- soft_queries: bfloat16 [2048, 8192], P(('groups', 'seq'), ('section', 'mp')), parts along dimension 0, may hold values from -150 to 150
- soft_keys: bfloat16 [2048, 1024], P(('groups', 'seq'), ('section', 'mp')), parts along dimension 0, may hold values from -6 to 6
- soft_values: bfloat16 [2048, 1024], P(('groups', 'seq'), ('section', 'mp')), parts along dimension 0, may hold values from -6 to 6
- lengths: int32 [8], P('groups'), parts along dimension 0, may hold values from 1 to 256, 768 in all
Outputs:
- light_out: bfloat16 [2048, 8192], P(('groups', 'seq'), ('section', 'mp')), parts along dimension 0
- soft_out: bfloat16 [2048, 8192], P(('groups', 'seq'), ('section', 'mp')), parts along dimension 0
There are 2 independent parts, one for each index of `groups`. A program takes and returns all parts, laid end to end along the dimension named above; an argument that names none is the same for every part. Nothing has to cross between parts.
Inputs may be any that keep to these rules, and one draw needn't show every extreme that they name: The live tokens of a block stand at its first slots; the lengths sum to 768.
All inputs are finite; a program needn't handle non-finite values.
Results may differ from a plain program's by a relative error of at most 0.007.
Values may be sent and summed in bfloat16 or wider, within the bound.
A program may use at most 64 MiB of HBM per device.

v0:
```python
import functools
import math

import jax
import jax.numpy as jnp
from jax import lax
from jax.experimental import pallas as pl
from jax.experimental.pallas import tpu as pltpu
from jax.sharding import PartitionSpec as P

MESH = pl.DeviceIdType.MESH
LOG2E = 1.4426950408889634
LOW = -1e30
CHUNK = 2
UNIT = 4
FINISH = 4


def mm(a, b, dims=((1,), (0,)), precision=None):
    return lax.dot_general(
        a, b, (dims, ((), ())), precision=precision, preferred_element_type=jnp.float32
    )


def kernel(
    n, width,
    lq_hbm, lk_hbm, lv_hbm, decay_hbm, gain_hbm, sq_hbm, sk_hbm, sv_hbm, lengths,
    light_out, soft_out,
    lq, lk, lv, sq, decay, gain, kbuf, vbuf,
    padded, cols, rows, states, state_in, state_out, bias, acc, peak,
    local_sem, k_send, k_recv, v_send, v_recv, s_send, s_recv,
):
    me = lax.axis_index("seq")
    right = {"seq": me + 1}
    heads, toks = decay.shape
    kv_count = kbuf.shape[2] // width
    group = heads // kv_count
    chunks = heads // CHUNK
    scale = width ** (-0.5)
    bf16, f32 = jnp.bfloat16, jnp.float32

    copies = [
        pltpu.make_async_copy(src, dst, local_sem.at[i])
        for i, (src, dst) in enumerate((
            (sk_hbm, kbuf.at[0]), (sv_hbm, vbuf.at[0]), (decay_hbm, decay), (lk_hbm, lk),
            (lv_hbm, lv), (sq_hbm, sq), (lq_hbm, lq), (gain_hbm, gain),
        ))
    ]
    for copy in copies:
        copy.start()

    barrier = pltpu.get_barrier_semaphore()

    @pl.when(me > 0)
    def _():
        pl.semaphore_signal(barrier, inc=1, device_id={"seq": me - 1}, device_id_type=MESH)

    @pl.when(me < n - 1)
    def _():
        pl.semaphore_signal(barrier, inc=1, device_id=right, device_id_type=MESH)

    inner = (me > 0) & (me < n - 1)

    @pl.when(inner)
    def _():
        pl.semaphore_wait(barrier, 2)

    @pl.when(jnp.logical_not(inner))
    def _():
        pl.semaphore_wait(barrier, 1)

    def key_copy(step):
        return pltpu.make_async_remote_copy(
            src_ref=kbuf.at[step], dst_ref=kbuf.at[step + 1],
            send_sem=k_send.at[step], recv_sem=k_recv.at[step + 1],
            device_id=right, device_id_type=MESH,
        )

    def value_copy(step):
        return pltpu.make_async_remote_copy(
            src_ref=vbuf.at[step], dst_ref=vbuf.at[step + 1],
            send_sem=v_send.at[step], recv_sem=v_recv.at[step + 1],
            device_id=right, device_id_type=MESH,
        )

    def state_copy(c):
        piece = pl.ds(c * CHUNK, CHUNK)
        return pltpu.make_async_remote_copy(
            src_ref=state_out.at[piece], dst_ref=state_in.at[piece],
            send_sem=s_send.at[c], recv_sem=s_recv.at[c],
            device_id=right, device_id_type=MESH,
        )

    copies[0].wait()
    copies[1].wait()

    @pl.when(me < n - 1)
    def _():
        key_copy(0).start()
        value_copy(0).start()

    copies[2].wait()
    own = lengths[me]
    tok_col = lax.broadcasted_iota(jnp.int32, (toks, width), 0)
    live = tok_col < own
    padded[...] = jnp.zeros_like(padded)
    tok_lane = lax.broadcasted_iota(jnp.int32, (heads, toks), 1)
    masked = jnp.where(tok_lane < own, decay[...], 0.0)
    at0 = lax.broadcasted_iota(jnp.int32, (toks, toks), 0)
    at1 = lax.broadcasted_iota(jnp.int32, (toks, toks), 1)
    padded[:heads, :] = mm(masked, (at0 <= at1).astype(f32), precision=lax.Precision.HIGHEST)
    padded[:heads, :] = padded[:heads, :] * LOG2E
    rows[...] = padded[:heads, :]
    running = padded[...].T
    for h in range(heads):
        cols[h] = jnp.broadcast_to(running[:, h : h + 1], (toks, width))

    copies[3].wait()
    copies[4].wait()

    def head_lanes(h):
        return pl.ds(pl.multiple_of(h * width, width), width)

    def block_states(c, carry):
        hs = [c * CHUNK + j for j in range(CHUNK)]
        faded = []
        for h in hs:
            col = cols[h]
            fading = jnp.where(live, jnp.exp2(col[toks - 1 : toks, :] - col), 0.0)
            faded.append((lk[:, head_lanes(h)].astype(f32) * fading).astype(bf16).T)
        found = [mm(x, lv[:, head_lanes(h)]) for h, x in zip(hs, faded)]
        for h, state in zip(hs, found):
            states[h] = state
            state_out[h] = state.astype(bf16)

        @pl.when(me == 0)
        def _():
            state_copy(c).start()

        return carry

    lax.fori_loop(0, chunks, block_states, 0)

    copies[5].wait()
    factor = scale * LOG2E
    bias[...] = jnp.where(at0 <= at1, 0.0, LOW)
    part = min(UNIT, group)
    pad = acc.shape[1] - width
    lane_pos = lax.broadcasted_iota(jnp.int32, (pad, toks), 1)

    def arrive(step):
        key_copy(step - 1).wait_recv()
        value_copy(step - 1).wait_recv()

    def attend(step, first):
        if not first:
            @pl.when(me == n - 1)
            def _():
                arrive(step)

            known = lengths[me - step]
            key_live = tok_col < known

        units = [(g, i) for g in range(kv_count) for i in range(group // part)]
        for u, (g, i) in enumerate(units):
            if u == len(units) // 2:
                @pl.when((me < n - 1) & (step < me))
                def _():
                    arrive(step + 1)
                    key_copy(step + 1).start()
                    value_copy(step + 1).start()

            if i == 0:
                lanes_g = slice(g * width, (g + 1) * width)
                if first:
                    keys = kbuf[0, :, lanes_g]
                    values = vbuf[0, :, lanes_g].T
                    counted = jnp.ones((pad, toks), bf16)
                else:
                    keys = kbuf[step, :, lanes_g].astype(f32)
                    keys = jnp.where(key_live, keys, keys[0:1, :]).astype(bf16)
                    values = vbuf[step, :, lanes_g].astype(f32)
                    values = jnp.where(key_live, values, 0.0).astype(bf16).T
                    counted = jnp.where(lane_pos < known, 1.0, 0.0).astype(bf16)
                values = jnp.concatenate([values, counted], axis=0)
            hs = [g * group + i * part + j for j in range(part)]
            scores = [mm(keys, sq[:, h * width : (h + 1) * width], ((1,), (1,))) for h in hs]
            if first:
                scores = [x + bias[...] for x in scores]
                peaks = [jnp.max(x, axis=0, keepdims=True) for x in scores]
            else:
                olds = [peak[h] for h in hs]
                peaks = [
                    jnp.maximum(o, jnp.max(x, axis=0, keepdims=True)) for o, x in zip(olds, scores)
                ]
            probs = [jnp.exp2((x - p) * factor).astype(bf16) for x, p in zip(scores, peaks)]
            sums = [mm(values, x) for x in probs]
            if not first:
                sums = [
                    jnp.exp2((o - p) * factor) * acc[h] + x
                    for h, o, p, x in zip(hs, olds, peaks, sums)
                ]
            for h, p, x in zip(hs, peaks, sums):
                peak[h] = p
                acc[h] = x

    attend(0, True)

    def later(step, carry):
        attend(step, False)
        return carry

    lax.fori_loop(1, me + 1, later, 0)

    def finish_soft(c, carry):
        hs = [c * FINISH + j for j in range(FINISH)]
        results = [(acc[h, :width, :] / acc[h, width : width + 1, :]).T for h in hs]
        for h, x in zip(hs, results):
            soft_out[:, head_lanes(h)] = jnp.where(live, x, 0.0).astype(bf16)
        return carry

    lax.fori_loop(0, heads // FINISH, finish_soft, 0)

    copies[6].wait()
    copies[7].wait()

    @pl.when(me == 0)
    def _():
        state_in[...] = jnp.zeros_like(state_in)

    bias[...] = jnp.where(at0 >= at1, math.log2(scale), LOW)
    half = toks // 2

    def lightning(c, carry):
        hs = [c * CHUNK + j for j in range(CHUNK)]
        queries = [lq[:, head_lanes(h)] for h in hs]
        faded = [cols[h] for h in hs]
        insides = []
        for top in (True, False):
            size = half if top else toks
            span = slice(0, half) if top else slice(half, toks)
            raw = [
                mm(q[span, :], lk[:size, head_lanes(h)], ((1,), (1,))) for h, q in zip(hs, queries)
            ]
            weights = []
            for h, col, x in zip(hs, faded, raw):
                wide = jnp.concatenate([col[span, :]] * (size // width), axis=1)
                gaps = (wide - rows[pl.ds(h, 1), :][:, :size]) + bias[span, :size]
                weights.append((x * jnp.exp2(gaps)).astype(bf16))
            insides.append([mm(w, lv[:size, head_lanes(h)]) for h, w in zip(hs, weights)])
        insides = [jnp.concatenate(x, axis=0) for x in zip(*insides)]
        drops = [jnp.exp2(col) * scale for col in faded]

        @pl.when(me > 0)
        def _():
            state_copy(c).wait_recv()

            @pl.when(me < n - 1)
            def _():
                for h in hs:
                    kept = jnp.exp2(cols[h, toks - 1 : toks, :])
                    state_out[h] = (kept * state_in[h].astype(f32) + states[h]).astype(bf16)
                state_copy(c).start()

        across = [mm(q, state_in[h]) for h, q in zip(hs, queries)]
        combined = [i + a * d for i, a, d in zip(insides, across, drops)]
        means = [jnp.mean(x * x, axis=1, keepdims=True) for x in combined]
        for h, x, mean in zip(hs, combined, means):
            normed = x * lax.rsqrt(mean + 1e-06) * gain[pl.ds(h, 1), :]
            light_out[:, head_lanes(h)] = jnp.where(live, normed, 0.0).astype(bf16)
        return carry

    lax.fori_loop(0, chunks, lightning, 0)

    @pl.when(me < n - 1)
    def _():
        def sent_blocks(step, carry):
            key_copy(step).wait_send()
            value_copy(step).wait_send()
            return carry

        lax.fori_loop(0, me + 1, sent_blocks, 0)

        def sent_states(c, carry):
            state_copy(c).wait_send()
            return carry

        lax.fori_loop(0, chunks, sent_states, 0)


def body(n, lq, lk, lv, decay, gain, sq, sk, sv, lengths):
    toks, heads = decay.shape
    width = lq.shape[1] // heads
    kv = sk.shape[1]
    chunks = heads // CHUNK
    bf16, f32 = jnp.bfloat16, jnp.float32
    out = jax.ShapeDtypeStruct(lq.shape, bf16)
    dma = pltpu.SemaphoreType.DMA
    anywhere = pl.BlockSpec(memory_space=pltpu.HBM)
    vmem = pl.BlockSpec(memory_space=pltpu.VMEM)
    light, soft = pl.pallas_call(
        functools.partial(kernel, n, width),
        out_shape=(out, out),
        in_specs=[anywhere] * 8 + [pl.BlockSpec(memory_space=pltpu.SMEM)],
        out_specs=(vmem, vmem),
        scratch_shapes=[
            pltpu.VMEM(lq.shape, bf16), pltpu.VMEM(lq.shape, bf16), pltpu.VMEM(lq.shape, bf16),
            pltpu.VMEM(sq.shape, bf16), pltpu.VMEM((heads, toks), f32),
            pltpu.VMEM((heads, width), f32),
            pltpu.VMEM((n, toks, kv), bf16), pltpu.VMEM((n, toks, kv), bf16),
            pltpu.VMEM((width, toks), f32), pltpu.VMEM((heads, toks, width), f32),
            pltpu.VMEM((heads, toks), f32),
            pltpu.VMEM((heads, width, width), f32),
            pltpu.VMEM((heads, width, width), bf16), pltpu.VMEM((heads, width, width), bf16),
            pltpu.VMEM((toks, toks), f32),
            pltpu.VMEM((heads, width + 16, toks), f32), pltpu.VMEM((heads, 1, toks), f32),
            dma((8,)), dma((n,)), dma((n,)), dma((n,)), dma((n,)), dma((chunks,)), dma((chunks,)),
        ],
        compiler_params=pltpu.CompilerParams(
            collective_id=0, has_side_effects=True, vmem_limit_bytes=64800000
        ),
        name="hybrid",
    )(lq, lk, lv, decay.T, gain.reshape(heads, width), sq, sk, sv, lengths)
    largest = jnp.finfo(bf16).max
    return tuple(jnp.minimum(x, largest) for x in (light, soft))


def solution(mesh):
    block = P(("groups", "seq"), ("section", "mp"))
    return jax.shard_map(
        functools.partial(body, mesh.shape["seq"]),
        mesh=mesh,
        in_specs=(block, block, block, block, P(("section", "mp")), block, block, block, P("groups")),
        out_specs=(block, block),
        check_vma=False,
    )
```

profile of v0, /device:TPU:24, one launch (start us, length us, event | category | flops | bytes accessed | tf_op | source)
XLA Modules:
  0.0 38.0 jit_solution(17068739512404148411)
XLA Ops:
  0.6 34.3 %hybrid.1 = (bf16[256,2048]{1,0:T(8,128)(2,1)}, bf16[256,2048]{1,0:T(8,128)(2,1)}) custom-call(bf16[256,2048]{1,0:T(8,128)(2,1)} %lq_hbm.1, bf16[256,2048]{1,0:T(8,128)(2,1)} %lk_hbm.1, bf16[256,2048]{1,0:T(8,128)(2,1)} %lv_hbm.1, f32[16,256]{1,0:T(8,128)} %bitcast.2, f32[16,128]{1,0:T(8,128)} %bitcast.3, bf16[256,2048]{1,0:T(8,128)(2,1)} %sq_hbm.1, ...), custom_call_target="tpu_custom_call" | custom-call | tf_op jit(solution)/shard_map/hybrid/pallas_call | solution.py:301
  34.9 3.0 %broadcast_minimum_fusion = (bf16[256,2048]{1,0:T(8,128)(2,1)}, bf16[256,2048]{1,0:T(8,128)(2,1)}) fusion(bf16[256,2048]{1,0:T(8,128)(2,1)} %get-tuple-element.5, bf16[256,2048]{1,0:T(8,128)(2,1)} %get-tuple-element.4), kind=kLoop, calls=%fused_computation | loop fusion | flops 1048576 | bytes 4194304 | tf_op jit(solution)/shard_map/min | solution.py:325
where the time goes:
time: 38.2 us; the launch traced here: 38 us
  Pallas kernels  34.3 us (90%)
  other arithmetic  3.04 us (8%)
  between operations  0.64 us (2%)
    pallas_call x1, Pallas kernels, body(): pl.pallas_call(functools.partial(kernel, n, width), out_shape=(out, out),...  34.3 us
    min x1, other arithmetic, body(): return tuple((jnp.minimum(x, largest) for x in (light, soft)))  3.04 us

commit v1 on v0

--- a/solution.py
+++ b/solution.py
@@ -294,7 +294,7 @@
     kv = sk.shape[1]
     chunks = heads // CHUNK
     bf16, f32 = jnp.bfloat16, jnp.float32
-    out = jax.ShapeDtypeStruct(lq.shape, bf16)
+    out = pltpu.VMEM(lq.shape, bf16)
     dma = pltpu.SemaphoreType.DMA
     anywhere = pl.BlockSpec(memory_space=pltpu.HBM)
     vmem = pl.BlockSpec(memory_space=pltpu.VMEM)
@@ -317,7 +317,7 @@
             dma((8,)), dma((n,)), dma((n,)), dma((n,)), dma((n,)), dma((chunks,)), dma((chunks,)),
         ],
         compiler_params=pltpu.CompilerParams(
-            collective_id=0, has_side_effects=True, vmem_limit_bytes=64800000
+            collective_id=0, has_side_effects=True, vmem_limit_bytes=58000000
         ),
         name="hybrid",
     )(lq, lk, lv, decay.T, gain.reshape(heads, width), sq, sk, sv, lengths)

time: 38.2 us -> 35.3 us (0.924)
  other arithmetic: 3.04 us -> 1.5 us
  Pallas kernels: 34.3 us -> 33 us
    min x1, other arithmetic: 3.04 us -> 1.5 us  [body(): return tuple((jnp.minimum(x, largest) for x in (light, soft)))]
    pallas_call x1, Pallas kernels: 34.3 us -> 33 us  [body(): pl.pallas_call(functools.partial(kernel, n, width), out_shape=(out, out),...]
where the time goes in v1:
time: 35.3 us; the launch traced here: 35.1 us
  Pallas kernels  33 us (93%)
  other arithmetic  1.5 us (4%)
  between operations  0.64 us (2%)
    pallas_call x1, Pallas kernels, body(): pl.pallas_call(functools.partial(kernel, n, width), out_shape=(out, out),...  33 us
    min x1, other arithmetic, body(): return tuple((jnp.minimum(x, largest) for x in (light, soft)))  1.5 us

profile of v1, /device:TPU:24, one launch (start us, length us, event | category | flops | bytes accessed | tf_op | source)
XLA Modules:
  0.0 35.1 jit_solution(3869548980975556297)
XLA Ops:
  0.6 33.0 %hybrid.1 = (bf16[256,2048]{1,0:T(8,128)(2,1)S(1)}, bf16[256,2048]{1,0:T(8,128)(2,1)S(1)}) custom-call(bf16[256,2048]{1,0:T(8,128)(2,1)} %lq_hbm.1, bf16[256,2048]{1,0:T(8,128)(2,1)} %lk_hbm.1, bf16[256,2048]{1,0:T(8,128)(2,1)} %lv_hbm.1, f32[16,256]{1,0:T(8,128)} %bitcast.2, f32[16,128]{1,0:T(8,128)} %bitcast.3, bf16[256,2048]{1,0:T(8,128)(2,1)} %sq_hbm.1, ...), custom_call_target="tpu_custom_call" | custom-call | tf_op jit(solution)/shard_map/hybrid/pallas_call | solution.py:301
  33.6 1.5 %broadcast_minimum_fusion = (bf16[256,2048]{1,0:T(8,128)(2,1)}, bf16[256,2048]{1,0:T(8,128)(2,1)}) fusion(bf16[256,2048]{1,0:T(8,128)(2,1)S(1)} %get-tuple-element.5, bf16[256,2048]{1,0:T(8,128)(2,1)S(1)} %get-tuple-element.4), kind=kLoop, calls=%fused_computation | loop fusion | flops 1048576 | bytes 4194304 | tf_op jit(solution)/shard_map/min | solution.py:325

commit v2 on v1

v2 whole, which is shorter than its diff:
```python
import functools
import math

import jax
import jax.numpy as jnp
from jax import lax
from jax.experimental import pallas as pl
from jax.experimental.pallas import tpu as pltpu
from jax.sharding import PartitionSpec as P

MESH = pl.DeviceIdType.MESH
LOG2E = 1.4426950408889634
LOW = -1e30
CHUNK = 2
PIECES = 8
UNIT = 4
FINISH = 4


def mm(a, b, dims=((1,), (0,)), precision=None):
    return lax.dot_general(
        a, b, (dims, ((), ())), precision=precision, preferred_element_type=jnp.float32
    )


def can_pack(n, toks, width, heads, kv):
    return n == 4 and toks == 2 * width and heads >= 2 * kv // width


def kernel(
    n, width,
    lq_hbm, lk_hbm, lv_hbm, decay_hbm, gain_hbm, sq_hbm, sk_hbm, sv_hbm, lengths,
    light_out, soft_out,
    lq, lk, lv, sq, decay, gain, kvbuf,
    padded, cols, rows, states, state_in, state_out, bias, causal, insum, acc, peak, pack, spare, later_q,
    local_sem, kv_send, kv_recv, s_send, s_recv, q_send, q_recv,
):
    me = lax.axis_index("seq")
    right = {"seq": me + 1}
    heads, toks = decay.shape
    kv = kvbuf.shape[2] // 2
    kv_count = kv // width
    rows_piece = toks // PIECES
    half = toks // 2
    packed = can_pack(n, toks, width, heads, kv)
    tiles = 2 * kv // width
    last = n - 1
    group = heads // kv_count
    chunks = heads // CHUNK
    scale = width ** (-0.5)
    bf16, f32 = jnp.bfloat16, jnp.float32

    copies = [
        pltpu.make_async_copy(src, dst, local_sem.at[i])
        for i, (src, dst) in enumerate((
            (sk_hbm, kvbuf.at[0, :, :kv]), (sv_hbm, kvbuf.at[0, :, kv:]), (decay_hbm, decay), (lk_hbm, lk),
            (lv_hbm, lv), (sq_hbm, sq), (lq_hbm, lq), (gain_hbm, gain),
        ))
    ]
    for copy in copies:
        copy.start()

    barrier = pltpu.get_barrier_semaphore()

    @pl.when(me > 0)
    def _():
        pl.semaphore_signal(barrier, inc=1, device_id={"seq": me - 1}, device_id_type=MESH)

    @pl.when(me < n - 1)
    def _():
        pl.semaphore_signal(barrier, inc=1, device_id=right, device_id_type=MESH)

    inner = (me > 0) & (me < n - 1)

    @pl.when(inner)
    def _():
        pl.semaphore_wait(barrier, 2)

    @pl.when(jnp.logical_not(inner))
    def _():
        pl.semaphore_wait(barrier, 1)

    def kv_copy(step, p):
        piece = pl.ds(p * rows_piece, rows_piece)
        return pltpu.make_async_remote_copy(
            src_ref=kvbuf.at[step, piece], dst_ref=kvbuf.at[step + 1, piece],
            send_sem=kv_send.at[step, p], recv_sem=kv_recv.at[step + 1, p],
            device_id=right, device_id_type=MESH,
        )

    def state_copy(h):
        return pltpu.make_async_remote_copy(
            src_ref=state_out.at[h], dst_ref=state_in.at[h],
            send_sem=s_send.at[h], recv_sem=s_recv.at[h],
            device_id=right, device_id_type=MESH,
        )

    def pack_copy(k):
        step, p = divmod(k, PIECES)
        piece = pl.ds(p * rows_piece, rows_piece)
        return pltpu.make_async_remote_copy(
            src_ref=pack.at[pl.ds((k - PIECES // 2) * rows_piece, rows_piece)],
            dst_ref=kvbuf.at[step + 1, piece],
            send_sem=kv_send.at[step, p], recv_sem=kv_recv.at[step + 1, p],
            device_id=right, device_id_type=MESH,
        )

    query_copy = pltpu.make_async_remote_copy(
        src_ref=lq_hbm.at[:half], dst_ref=later_q, send_sem=q_send, recv_sem=q_recv,
        device_id={"seq": me - 1}, device_id_type=MESH,
    )
    packs = (me == n - 2) if packed else False
    unpacks = (me == last) if packed else False
    forwards = (me < n - 2) if packed else (me < last)

    if packed:
        @pl.when(unpacks)
        def _():
            query_copy.start()

    copies[0].wait()
    copies[1].wait()

    @pl.when(me < last)
    def _():
        for p in range(PIECES // 2):
            kv_copy(0, p).start()

    @pl.when(forwards)
    def _():
        for p in range(PIECES // 2, PIECES):
            kv_copy(0, p).start()

    copies[2].wait()
    own = lengths[me]
    if packed:
        ends = [lengths[b] for b in range(n)]
        short = ends[3] < half
        cut1 = jnp.where(short, ends[2] + ends[3] - toks, jnp.maximum(ends[2] - half, 0))
        cut0 = 2 * toks - ends[0]
    tok_col = lax.broadcasted_iota(jnp.int32, (toks, width), 0)
    live = tok_col < own
    padded[...] = jnp.zeros_like(padded)
    tok_lane = lax.broadcasted_iota(jnp.int32, (heads, toks), 1)
    masked = jnp.where(tok_lane < own, decay[...], 0.0)
    at0 = lax.broadcasted_iota(jnp.int32, (toks, toks), 0)
    at1 = lax.broadcasted_iota(jnp.int32, (toks, toks), 1)
    padded[:heads, :] = mm(masked, (at0 <= at1).astype(f32), precision=lax.Precision.HIGHEST)
    padded[:heads, :] = padded[:heads, :] * LOG2E
    rows[...] = padded[:heads, :]
    running = padded[...].T
    for h in range(heads):
        cols[h] = jnp.broadcast_to(running[:, h : h + 1], (toks, width))

    copies[3].wait()
    copies[4].wait()

    def head_lanes(h):
        return pl.ds(h * width if isinstance(h, int) else pl.multiple_of(h * width, width), width)

    def block_states(hs):
        faded = []
        for h in hs:
            col = cols[h]
            fading = jnp.where(live, jnp.exp2(col[toks - 1 : toks, :] - col), 0.0)
            faded.append((lk[:, head_lanes(h)].astype(f32) * fading).astype(bf16).T)
        found = [mm(x, lv[:, head_lanes(h)]) for h, x in zip(hs, faded)]
        for h, state in zip(hs, found):
            states[h] = state
            state_out[h] = state.astype(bf16)

    def insides(hs):
        parts = []
        for top in (True, False):
            size = half if top else toks
            span = slice(0, half) if top else slice(half, toks)
            raw = [mm(lq[span, head_lanes(h)], lk[:size, head_lanes(h)], ((1,), (1,))) for h in hs]
            weights = []
            for h, x in zip(hs, raw):
                wide = jnp.concatenate([cols[h, span, :]] * (size // width), axis=1)
                gaps = (wide - rows[h : h + 1, :size]) + causal[span, :size]
                weights.append((x * jnp.exp2(gaps)).astype(bf16))
            parts.append([mm(w, lv[:size, head_lanes(h)]) for h, w in zip(hs, weights)])
        for h, top, low in zip(hs, *parts):
            insum[h, :half, :] = top
            insum[h, half:, :] = low

    copies[5].wait()
    copies[6].wait()
    factor = scale * LOG2E
    bias[...] = jnp.where(at0 <= at1, 0.0, LOW)
    causal[...] = jnp.where(at0 >= at1, math.log2(scale), LOW)
    part = min(UNIT, group)
    units = heads // part
    pad = acc.shape[1] - width
    lane_pos = lax.broadcasted_iota(jnp.int32, (pad, toks), 1)

    def one_hot(size, span, shift, limit):
        dst = lax.broadcasted_iota(jnp.int32, (size, span), 0)
        src = lax.broadcasted_iota(jnp.int32, (size, span), 1)
        return jnp.where((src - dst == shift) & (src < limit), 1.0, 0.0).astype(bf16)

    def fill(j):
        start = j * rows_piece
        total = jnp.zeros((rows_piece, 2 * kv), f32)
        if start < half:
            at = lax.broadcasted_iota(jnp.int32, (rows_piece, 2 * kv), 0) + start
            tail = kvbuf[0, half + start : half + start + rows_piece, :].astype(f32)
            total = jnp.where(at < cut1, tail, total)
        low, high = max(0, start - half), min(toks, start + rows_piece)
        if low < high:
            hot = one_hot(rows_piece, high - low, start - low - cut1, ends[1] - low)
            total = total + mm(hot, kvbuf[1, low:high, :])
        if start >= toks:
            high = start - toks + rows_piece
            total = total + mm(one_hot(rows_piece, high, start - cut0, high), kvbuf[2, :high, :])
        pack[start : start + rows_piece, :] = total.astype(bf16)

    def arrive(step, u):
        each = PIECES // units
        for p in range(u * each, (u + 1) * each):
            needed = True if not packed else (me < last) | (step < last) | (p < PIECES // 2)

            @pl.when(needed)
            def _():
                kv_copy(step - 1, p).wait_recv()

            @pl.when(forwards)
            def _():
                kv_copy(step, p).start()

            if packed:
                for b in (1, 2) if not isinstance(step, int) else (step,):
                    @pl.when(packs & (step == b))
                    def _():
                        j = (b - 1) * PIECES + p
                        fill(j)
                        pack_copy(PIECES // 2 + j).start()

    def pass_states(hs):
        for h in hs:
            state_copy(h).wait_recv()
            kept = jnp.exp2(cols[h, toks - 1 : toks, :])
            state_out[h] = (kept * state_in[h].astype(f32) + states[h]).astype(bf16)
            if packed:
                @pl.when(packs)
                def _():
                    out = state_out[h]
                    found = mm(later_q[:, head_lanes(h)], out)
                    extra = spare[jnp.minimum(h, tiles - 1)]
                    out = jnp.where(state_row < spare_end, extra, out.astype(f32))
                    state_out[h] = jnp.where(state_row < result_end, found, out).astype(bf16)

            state_copy(h).start()

    def unpack():
        for h in range(tiles):
            state_copy(h).wait_recv()
        for h in range(tiles):
            kvbuf[last, half:, h * width : (h + 1) * width] = state_in[h]

    def ranges(step):
        if not packed:
            return lengths[me - step], toks, toks, toks
        flat = lengths[jnp.maximum(me - step, 0)]
        joint = cut1 + ends[1]
        at = [step == k for k in range(n)]

        def pick(plain, one, two, three):
            return jnp.where(unpacks, jnp.where(at[1], one, jnp.where(at[2], two, three)), plain)

        return (
            pick(flat, jnp.minimum(ends[2], half), joint - half, jnp.minimum(joint - toks - half, half)),
            pick(toks, half, toks, cut0 - toks - half),
            pick(toks, half + joint, toks, half),
            pick(toks, toks, cut0 - half, jnp.where(short, half + ends[3], toks)),
        )

    def within(at, limits):
        a, b, c, d = limits
        return (at < a) | ((at >= b) & (at < c)) | (at >= d)

    def attend(step, u, shared):
        first = isinstance(step, int)
        g, i = divmod(u, group // part)
        if i == 0:
            lanes_g = slice(g * width, (g + 1) * width)
            lanes_v = slice(kv + g * width, kv + (g + 1) * width)
            if first:
                keys = kvbuf[0, :, lanes_g]
                values = kvbuf[0, :, lanes_v].T
                counted = jnp.ones((pad, toks), bf16)
            else:
                limits = ranges(step)
                key_live = within(tok_col, limits)
                seen = kvbuf[0, 0:1, lanes_g].astype(f32)
                keys = kvbuf[step, :, lanes_g].astype(f32)
                keys = jnp.where(key_live, keys, seen).astype(bf16)
                values = kvbuf[step, :, lanes_v].astype(f32)
                values = jnp.where(key_live, values, 0.0).astype(bf16).T
                counted = jnp.where(within(lane_pos, limits), 1.0, 0.0).astype(bf16)
            shared[:] = [keys, jnp.concatenate([values, counted], axis=0)]
        keys, values = shared
        hs = [g * group + i * part + j for j in range(part)]
        scores = [mm(keys, sq[:, h * width : (h + 1) * width], ((1,), (1,))) for h in hs]
        if first:
            scores = [x + bias[...] for x in scores]
            peaks = [jnp.max(x, axis=0, keepdims=True) for x in scores]
        else:
            olds = [peak[h] for h in hs]
            peaks = [
                jnp.maximum(o, jnp.max(x, axis=0, keepdims=True)) for o, x in zip(olds, scores)
            ]
        probs = [jnp.exp2((x - p) * factor).astype(bf16) for x, p in zip(scores, peaks)]
        sums = [mm(values, x) for x in probs]
        if not first:
            sums = [
                jnp.exp2((o - p) * factor) * acc[h] + x
                for h, o, p, x in zip(hs, olds, peaks, sums)
            ]
        for h, p, x in zip(hs, peaks, sums):
            peak[h] = p
            acc[h] = x

    shared = []
    for u in range(units):
        @pl.when(me > 0)
        def _():
            arrive(1, u)

        attend(0, u, shared)
        hs = range(u * part, (u + 1) * part)
        block_states(hs)
        insides(hs)

        @pl.when(me == 0)
        def _():
            for h in hs:
                state_copy(h).start()

    if packed:
        state_row = lax.broadcasted_iota(jnp.int32, (width, width), 0)
        result_end = jnp.where(short, ends[3], 0)
        spare_end = jnp.where(short, width, 0)
        across_end = jnp.where(unpacks & short, half, 0)

    relays = (me > 0) & (me < last)
    early = heads // 2

    def later(step, carry):
        if packed:
            @pl.when(unpacks & (step == last))
            def _():
                unpack()

            @pl.when(packs & (step == me))
            def _():
                query_copy.wait_recv()
                moved = mm(one_hot(half, toks, ends[2] - half, toks), kvbuf[0])
                for h in range(tiles):
                    spare[h] = moved[:, h * width : (h + 1) * width]

        shared = []
        for u in range(units):
            @pl.when(step < me)
            def _():
                arrive(step + 1, u)

            @pl.when(relays & (step == me))
            def _():
                each = early // units
                pass_states(range(u * each, (u + 1) * each))

            attend(step, u, shared)
        return carry

    lax.fori_loop(1, me + 1, later, 0)

    def finish_soft(c, carry):
        hs = [c * FINISH + j for j in range(FINISH)]
        results = [(acc[h, :width, :] / acc[h, width : width + 1, :]).T for h in hs]
        for h, x in zip(hs, results):
            soft_out[:, head_lanes(h)] = jnp.where(live, x, 0.0).astype(bf16)
        return carry

    lax.fori_loop(0, heads // FINISH, finish_soft, 0)

    copies[7].wait()

    @pl.when(me == 0)
    def _():
        state_in[...] = jnp.zeros_like(state_in)

    def lightning(c, carry):
        hs = [c * CHUNK + j for j in range(CHUNK)]

        @pl.when(relays & (c < chunks // 2))
        def _():
            pass_states([h + early for h in hs])

        @pl.when((me == last) & (c >= tiles // CHUNK if packed else True))
        def _():
            for h in hs:
                state_copy(h).wait_recv()

        across = [mm(lq[:, head_lanes(h)], state_in[h]) for h in hs]
        if packed:
            results = [state_in[h].astype(f32) for h in hs]
            results = [jnp.concatenate([x] * (toks // width), axis=0) for x in results]
            across = [jnp.where(tok_col < across_end, x, y) for x, y in zip(results, across)]
        drops = [jnp.exp2(cols[h]) * scale for h in hs]
        combined = [insum[h] + a * d for h, a, d in zip(hs, across, drops)]
        means = [jnp.mean(x * x, axis=1, keepdims=True) for x in combined]
        for h, x, mean in zip(hs, combined, means):
            normed = x * lax.rsqrt(mean + 1e-06) * gain[pl.ds(h, 1), :]
            light_out[:, head_lanes(h)] = jnp.where(live, normed, 0.0).astype(bf16)
        return carry

    lax.fori_loop(0, chunks, lightning, 0)

    if packed:
        @pl.when(unpacks)
        def _():
            query_copy.wait_send()

    @pl.when(me < n - 1)
    def _():
        def sent_blocks(step, carry):
            for p in range(PIECES):
                sent = True if not packed else (me < n - 2) | (step < n - 2) | (p < PIECES // 2)

                @pl.when(sent)
                def _():
                    kv_copy(step, p).wait_send()

            return carry

        lax.fori_loop(0, me + 1, sent_blocks, 0)

        def sent_states(h, carry):
            state_copy(h).wait_send()
            return carry

        lax.fori_loop(0, heads, sent_states, 0)


def body(n, lq, lk, lv, decay, gain, sq, sk, sv, lengths):
    toks, heads = decay.shape
    width = lq.shape[1] // heads
    kv = sk.shape[1]
    chunks = heads // CHUNK
    bf16, f32 = jnp.bfloat16, jnp.float32
    out = pltpu.VMEM(lq.shape, bf16)
    dma = pltpu.SemaphoreType.DMA
    anywhere = pl.BlockSpec(memory_space=pltpu.HBM)
    vmem = pl.BlockSpec(memory_space=pltpu.VMEM)
    light, soft = pl.pallas_call(
        functools.partial(kernel, n, width),
        out_shape=(out, out),
        in_specs=[anywhere] * 8 + [pl.BlockSpec(memory_space=pltpu.SMEM)],
        out_specs=(vmem, vmem),
        scratch_shapes=[
            pltpu.VMEM(lq.shape, bf16), pltpu.VMEM(lq.shape, bf16), pltpu.VMEM(lq.shape, bf16),
            pltpu.VMEM(sq.shape, bf16), pltpu.VMEM((heads, toks), f32),
            pltpu.VMEM((heads, width), f32),
            pltpu.VMEM((n, toks, 2 * kv), bf16),
            pltpu.VMEM((width, toks), f32), pltpu.VMEM((heads, toks, width), f32),
            pltpu.VMEM((heads, toks), f32),
            pltpu.VMEM((heads, width, width), f32),
            pltpu.VMEM((heads, width, width), bf16), pltpu.VMEM((heads, width, width), bf16),
            pltpu.VMEM((toks, toks), f32), pltpu.VMEM((toks, toks), f32),
            pltpu.VMEM((heads, toks, width), f32),
            pltpu.VMEM((heads, width + 16, toks), f32), pltpu.VMEM((heads, 1, toks), f32),
            pltpu.VMEM((2 * toks, 2 * kv), bf16), pltpu.VMEM((2 * kv // width, toks // 2, width), f32),
            pltpu.VMEM((toks // 2, lq.shape[1]), bf16),
            dma((8,)), dma((n, PIECES)), dma((n, PIECES)), dma((heads,)), dma((heads,)), dma, dma,
        ],
        compiler_params=pltpu.CompilerParams(
            collective_id=0, has_side_effects=True, vmem_limit_bytes=58000000
        ),
        name="hybrid",
    )(lq, lk, lv, decay.T, gain.reshape(heads, width), sq, sk, sv, lengths)
    largest = jnp.finfo(bf16).max
    return tuple(jnp.minimum(x, largest) for x in (light, soft))


def solution(mesh):
    block = P(("groups", "seq"), ("section", "mp"))
    return jax.shard_map(
        functools.partial(body, mesh.shape["seq"]),
        mesh=mesh,
        in_specs=(block, block, block, block, P(("section", "mp")), block, block, block, P("groups")),
        out_specs=(block, block),
        check_vma=False,
    )
```

time: 35.3 us -> 32.7 us (0.926)
  Pallas kernels: 33 us -> 30.4 us
    pallas_call x1, Pallas kernels: 33 us -> 30.4 us  [body(): pl.pallas_call(functools.partial(kernel, n, width), out_shape=(out, out),...]
where the time goes in v2:
time: 32.7 us; the launch traced here: 32.5 us
  Pallas kernels  30.4 us (93%)
  other arithmetic  1.5 us (5%)
  between operations  0.64 us (2%)
    pallas_call x1, Pallas kernels, body(): pl.pallas_call(functools.partial(kernel, n, width), out_shape=(out, out),...  30.4 us
    min x1, other arithmetic, body(): return tuple((jnp.minimum(x, largest) for x in (light, soft)))  1.5 us

profile of v2, /device:TPU:24, one launch (start us, length us, event | category | flops | bytes accessed | tf_op | source)
XLA Modules:
  0.0 32.5 jit_solution(6561637043000454120)
XLA Ops:
  0.6 30.4 %hybrid.1 = (bf16[256,2048]{1,0:T(8,128)(2,1)S(1)}, bf16[256,2048]{1,0:T(8,128)(2,1)S(1)}) custom-call(bf16[256,2048]{1,0:T(8,128)(2,1)} %lq_hbm.1, bf16[256,2048]{1,0:T(8,128)(2,1)} %lk_hbm.1, bf16[256,2048]{1,0:T(8,128)(2,1)} %lv_hbm.1, f32[16,256]{1,0:T(8,128)} %bitcast.2, f32[16,128]{1,0:T(8,128)} %bitcast.3, bf16[256,2048]{1,0:T(8,128)(2,1)} %sq_hbm.1, ...), custom_call_target="tpu_custom_call" | custom-call | tf_op jit(solution)/shard_map/hybrid/pallas_call | solution.py:457
  31.0 1.5 %broadcast_minimum_fusion = (bf16[256,2048]{1,0:T(8,128)(2,1)}, bf16[256,2048]{1,0:T(8,128)(2,1)}) fusion(bf16[256,2048]{1,0:T(8,128)(2,1)S(1)} %get-tuple-element.5, bf16[256,2048]{1,0:T(8,128)(2,1)S(1)} %get-tuple-element.4), kind=kLoop, calls=%fused_computation | loop fusion | flops 1048576 | bytes 4194304 | tf_op jit(solution)/shard_map/min | solution.py:484

commit v3 on v2

--- a/solution.py
+++ b/solution.py
@@ -12,7 +12,8 @@
 LOG2E = 1.4426950408889634
 LOW = -1e30
 CHUNK = 2
-PIECES = 8
+PIECES = 4
+BATCH = 2
 UNIT = 4
 FINISH = 4
 
@@ -29,9 +30,9 @@
 
 def kernel(
     n, width,
-    lq_hbm, lk_hbm, lv_hbm, decay_hbm, gain_hbm, sq_hbm, sk_hbm, sv_hbm, lengths,
+    lq_hbm, lk_hbm, lv_hbm, decay_hbm, gain_hbm, sq_hbm, sk_hbm, sv_hbm, lengths_hbm,
     light_out, soft_out,
-    lq, lk, lv, sq, decay, gain, kvbuf,
+    lengths, lq, lk, lv, sq, decay, gain, kvbuf,
     padded, cols, rows, states, state_in, state_out, bias, causal, insum, acc, peak, pack, spare, later_q,
     local_sem, kv_send, kv_recv, s_send, s_recv, q_send, q_recv,
 ):
@@ -55,6 +56,7 @@
         for i, (src, dst) in enumerate((
             (sk_hbm, kvbuf.at[0, :, :kv]), (sv_hbm, kvbuf.at[0, :, kv:]), (decay_hbm, decay), (lk_hbm, lk),
             (lv_hbm, lv), (sq_hbm, sq), (lq_hbm, lq), (gain_hbm, gain),
+            (lengths_hbm, lengths),
         ))
     ]
     for copy in copies:
@@ -66,17 +68,12 @@
     def _():
         pl.semaphore_signal(barrier, inc=1, device_id={"seq": me - 1}, device_id_type=MESH)
 
-    @pl.when(me < n - 1)
-    def _():
-        pl.semaphore_signal(barrier, inc=1, device_id=right, device_id_type=MESH)
-
-    inner = (me > 0) & (me < n - 1)
-
-    @pl.when(inner)
-    def _():
-        pl.semaphore_wait(barrier, 2)
-
-    @pl.when(jnp.logical_not(inner))
+    if packed:
+        @pl.when(me == n - 2)
+        def _():
+            pl.semaphore_signal(barrier, inc=1, device_id=right, device_id_type=MESH)
+
+    @pl.when(True if packed else me < n - 1)
     def _():
         pl.semaphore_wait(barrier, 1)
 
@@ -88,10 +85,11 @@
             device_id=right, device_id_type=MESH,
         )
 
-    def state_copy(h):
+    def state_copy(b):
+        batch = pl.ds(b * BATCH, BATCH)
         return pltpu.make_async_remote_copy(
-            src_ref=state_out.at[h], dst_ref=state_in.at[h],
-            send_sem=s_send.at[h], recv_sem=s_recv.at[h],
+            src_ref=state_out.at[batch], dst_ref=state_in.at[batch],
+            send_sem=s_send.at[b], recv_sem=s_recv.at[b],
             device_id=right, device_id_type=MESH,
         )
 
@@ -132,6 +130,7 @@
             kv_copy(0, p).start()
 
     copies[2].wait()
+    copies[8].wait()
     own = lengths[me]
     if packed:
         ends = [lengths[b] for b in range(n)]
@@ -237,25 +236,29 @@
                         fill(j)
                         pack_copy(PIECES // 2 + j).start()
 
-    def pass_states(hs):
-        for h in hs:
-            state_copy(h).wait_recv()
-            kept = jnp.exp2(cols[h, toks - 1 : toks, :])
-            state_out[h] = (kept * state_in[h].astype(f32) + states[h]).astype(bf16)
-            if packed:
-                @pl.when(packs)
-                def _():
-                    out = state_out[h]
-                    found = mm(later_q[:, head_lanes(h)], out)
+    def pass_states(b):
+        hs = [b * BATCH + j for j in range(BATCH)]
+        state_copy(b).wait_recv()
+        kept = [jnp.exp2(cols[h, toks - 1 : toks, :]) for h in hs]
+        left = [(k * state_in[h].astype(f32) + states[h]).astype(bf16) for h, k in zip(hs, kept)]
+        for h, x in zip(hs, left):
+            state_out[h] = x
+
+        if packed:
+            @pl.when(packs)
+            def _():
+                outs = [state_out[h] for h in hs]
+                found = [mm(later_q[:, head_lanes(h)], x) for h, x in zip(hs, outs)]
+                for h, x, y in zip(hs, outs, found):
                     extra = spare[jnp.minimum(h, tiles - 1)]
-                    out = jnp.where(state_row < spare_end, extra, out.astype(f32))
-                    state_out[h] = jnp.where(state_row < result_end, found, out).astype(bf16)
-
-            state_copy(h).start()
+                    x = jnp.where(state_row < spare_end, extra, x.astype(f32))
+                    state_out[h] = jnp.where(state_row < result_end, y, x).astype(bf16)
+
+        state_copy(b).start()
 
     def unpack():
-        for h in range(tiles):
-            state_copy(h).wait_recv()
+        for b in range(tiles // BATCH):
+            state_copy(b).wait_recv()
         for h in range(tiles):
             kvbuf[last, half:, h * width : (h + 1) * width] = state_in[h]
 
@@ -335,8 +338,8 @@
 
         @pl.when(me == 0)
         def _():
-            for h in hs:
-                state_copy(h).start()
+            for b in range(u * part // BATCH, (u + 1) * part // BATCH):
+                state_copy(b).start()
 
     if packed:
         state_row = lax.broadcasted_iota(jnp.int32, (width, width), 0)
@@ -368,8 +371,9 @@
 
             @pl.when(relays & (step == me))
             def _():
-                each = early // units
-                pass_states(range(u * each, (u + 1) * each))
+                each = early // BATCH // units
+                for b in range(u * each, (u + 1) * each):
+                    pass_states(b)
 
             attend(step, u, shared)
         return carry
@@ -396,12 +400,13 @@
 
         @pl.when(relays & (c < chunks // 2))
         def _():
-            pass_states([h + early for h in hs])
+            for j in range(CHUNK // BATCH):
+                pass_states((c * CHUNK + early) // BATCH + j)
 
         @pl.when((me == last) & (c >= tiles // CHUNK if packed else True))
         def _():
-            for h in hs:
-                state_copy(h).wait_recv()
+            for j in range(CHUNK // BATCH):
+                state_copy(c * (CHUNK // BATCH) + j).wait_recv()
 
         across = [mm(lq[:, head_lanes(h)], state_in[h]) for h in hs]
         if packed:
@@ -437,11 +442,11 @@
 
         lax.fori_loop(0, me + 1, sent_blocks, 0)
 
-        def sent_states(h, carry):
-            state_copy(h).wait_send()
+        def sent_states(b, carry):
+            state_copy(b).wait_send()
             return carry
 
-        lax.fori_loop(0, heads, sent_states, 0)
+        lax.fori_loop(0, heads // BATCH, sent_states, 0)
 
 
 def body(n, lq, lk, lv, decay, gain, sq, sk, sv, lengths):
@@ -457,9 +462,10 @@
     light, soft = pl.pallas_call(
         functools.partial(kernel, n, width),
         out_shape=(out, out),
-        in_specs=[anywhere] * 8 + [pl.BlockSpec(memory_space=pltpu.SMEM)],
+        in_specs=[anywhere] * 9,
         out_specs=(vmem, vmem),
         scratch_shapes=[
+            pltpu.SMEM(lengths.shape, lengths.dtype),
             pltpu.VMEM(lq.shape, bf16), pltpu.VMEM(lq.shape, bf16), pltpu.VMEM(lq.shape, bf16),
             pltpu.VMEM(sq.shape, bf16), pltpu.VMEM((heads, toks), f32),
             pltpu.VMEM((heads, width), f32),
@@ -473,7 +479,7 @@
             pltpu.VMEM((heads, width + 16, toks), f32), pltpu.VMEM((heads, 1, toks), f32),
             pltpu.VMEM((2 * toks, 2 * kv), bf16), pltpu.VMEM((2 * kv // width, toks // 2, width), f32),
             pltpu.VMEM((toks // 2, lq.shape[1]), bf16),
-            dma((8,)), dma((n, PIECES)), dma((n, PIECES)), dma((heads,)), dma((heads,)), dma, dma,
+            dma((9,)), dma((n, PIECES)), dma((n, PIECES)), dma((heads // BATCH,)), dma((heads // BATCH,)), dma, dma,
         ],
         compiler_params=pltpu.CompilerParams(
             collective_id=0, has_side_effects=True, vmem_limit_bytes=58000000

time: 32.7 us -> 31.4 us (0.960)
  Pallas kernels: 30.4 us -> 29.1 us
    pallas_call x1, Pallas kernels: 30.4 us -> 29.1 us  [body(): pl.pallas_call(functools.partial(kernel, n, width), out_shape=(out, out),...]
where the time goes in v3:
time: 31.4 us; the launch traced here: 31.3 us
  Pallas kernels  29.1 us (93%)
  other arithmetic  1.5 us (5%)
  between operations  0.64 us (2%)
    pallas_call x1, Pallas kernels, body(): pl.pallas_call(functools.partial(kernel, n, width), out_shape=(out, out),...  29.1 us
    min x1, other arithmetic, body(): return tuple((jnp.minimum(x, largest) for x in (light, soft)))  1.5 us

profile of v3, /device:TPU:24, one launch (start us, length us, event | category | flops | bytes accessed | tf_op | source)
XLA Modules:
  0.0 31.3 jit_solution(18252963319275349042)
XLA Ops:
  0.6 29.1 %hybrid.1 = (bf16[256,2048]{1,0:T(8,128)(2,1)S(1)}, bf16[256,2048]{1,0:T(8,128)(2,1)S(1)}) custom-call(bf16[256,2048]{1,0:T(8,128)(2,1)} %lq_hbm.1, bf16[256,2048]{1,0:T(8,128)(2,1)} %lk_hbm.1, bf16[256,2048]{1,0:T(8,128)(2,1)} %lv_hbm.1, f32[16,256]{1,0:T(8,128)} %bitcast.2, f32[16,128]{1,0:T(8,128)} %bitcast.3, bf16[256,2048]{1,0:T(8,128)(2,1)} %sq_hbm.1, ...), custom_call_target="tpu_custom_call" | custom-call | tf_op jit(solution)/shard_map/hybrid/pallas_call | solution.py:462
  29.8 1.5 %broadcast_minimum_fusion = (bf16[256,2048]{1,0:T(8,128)(2,1)}, bf16[256,2048]{1,0:T(8,128)(2,1)}) fusion(bf16[256,2048]{1,0:T(8,128)(2,1)S(1)} %get-tuple-element.5, bf16[256,2048]{1,0:T(8,128)(2,1)S(1)} %get-tuple-element.4), kind=kLoop, calls=%fused_computation | loop fusion | flops 1048576 | bytes 4194304 | tf_op jit(solution)/shard_map/min | solution.py:490

commit v4 on v3

--- a/solution.py
+++ b/solution.py
@@ -31,7 +31,7 @@
 def kernel(
     n, width,
     lq_hbm, lk_hbm, lv_hbm, decay_hbm, gain_hbm, sq_hbm, sk_hbm, sv_hbm, lengths_hbm,
-    light_out, soft_out,
+    light_out, soft_out, end_q, end_state, end_sum, end_drop, end_mask, end_gain,
     lengths, lq, lk, lv, sq, decay, gain, kvbuf,
     padded, cols, rows, states, state_in, state_out, bias, causal, insum, acc, peak, pack, spare, later_q,
     local_sem, kv_send, kv_recv, s_send, s_recv, q_send, q_recv,
@@ -395,6 +395,15 @@
     def _():
         state_in[...] = jnp.zeros_like(state_in)
 
+    ends_at = heads - CHUNK
+    end_q[...] = lq[:, ends_at * width :]
+    for j in range(CHUNK):
+        end_sum[j] = insum[ends_at + j]
+        end_drop[j] = jnp.exp2(cols[ends_at + j]) * scale
+    end_gain[...] = gain[ends_at:, :]
+    mask = jnp.where(live, 1.0, 0.0)
+    end_mask[...] = jnp.where(tok_col < across_end, mask + 2.0, mask) if packed else mask
+
     def lightning(c, carry):
         hs = [c * CHUNK + j for j in range(CHUNK)]
 
@@ -421,7 +430,15 @@
             light_out[:, head_lanes(h)] = jnp.where(live, normed, 0.0).astype(bf16)
         return carry
 
-    lax.fori_loop(0, chunks, lightning, 0)
+    lax.fori_loop(0, chunks - 1, lightning, 0)
+
+    @pl.when(me == last)
+    def _():
+        for j in range(CHUNK // BATCH):
+            state_copy(ends_at // BATCH + j).wait_recv()
+
+    for j in range(CHUNK):
+        end_state[j] = state_in[ends_at + j]
 
     if packed:
         @pl.when(unpacks)
@@ -447,6 +464,37 @@
             return carry
 
         lax.fori_loop(0, heads // BATCH, sent_states, 0)
+
+
+def finish(
+    light, soft, end_q, end_state, end_sum, end_drop, end_mask, end_gain,
+    light_hbm, soft_hbm, ready, sem,
+):
+    toks, width = end_mask.shape
+    done = light.shape[1] - end_q.shape[1]
+    f32 = jnp.float32
+    copies = [
+        pltpu.make_async_copy(soft, soft_hbm, sem.at[0]),
+        pltpu.make_async_copy(light.at[:, :done], light_hbm.at[:, :done], sem.at[1]),
+        pltpu.make_async_copy(ready, light_hbm.at[:, done:], sem.at[2]),
+    ]
+    copies[0].start()
+    copies[1].start()
+    mask = end_mask[...]
+    spans = [slice(j * width, (j + 1) * width) for j in range(CHUNK)]
+    across = [mm(end_q[:, span], end_state[j]) for j, span in enumerate(spans)]
+    given = [end_state[j].astype(f32) for j in range(CHUNK)]
+    given = [jnp.concatenate([x] * (toks // width), axis=0) for x in given]
+    across = [jnp.where(mask > 1.5, x, y) for x, y in zip(given, across)]
+    combined = [end_sum[j] + x * end_drop[j] for j, x in enumerate(across)]
+    means = [jnp.mean(x * x, axis=1, keepdims=True) for x in combined]
+    live = (mask == 1.0) | (mask == 3.0)
+    for j, (x, mean) in enumerate(zip(combined, means)):
+        normed = x * lax.rsqrt(mean + 1e-06) * end_gain[j : j + 1, :]
+        ready[:, spans[j]] = jnp.where(live, normed, 0.0).astype(jnp.bfloat16)
+    copies[2].start()
+    for copy in copies:
+        copy.wait()
 
 
 def body(n, lq, lk, lv, decay, gain, sq, sk, sv, lengths):
@@ -459,11 +507,16 @@
     dma = pltpu.SemaphoreType.DMA
     anywhere = pl.BlockSpec(memory_space=pltpu.HBM)
     vmem = pl.BlockSpec(memory_space=pltpu.VMEM)
-    light, soft = pl.pallas_call(
+    ends = CHUNK * width
+    left = pl.pallas_call(
         functools.partial(kernel, n, width),
-        out_shape=(out, out),
+        out_shape=(
+            out, out, pltpu.VMEM((toks, ends), bf16), pltpu.VMEM((CHUNK, width, width), bf16),
+            pltpu.VMEM((CHUNK, toks, width), f32), pltpu.VMEM((CHUNK, toks, width), f32),
+            pltpu.VMEM((toks, width), f32), pltpu.VMEM((CHUNK, width), f32),
+        ),
         in_specs=[anywhere] * 9,
-        out_specs=(vmem, vmem),
+        out_specs=(vmem,) * 8,
         scratch_shapes=[
             pltpu.SMEM(lengths.shape, lengths.dtype),
             pltpu.VMEM(lq.shape, bf16), pltpu.VMEM(lq.shape, bf16), pltpu.VMEM(lq.shape, bf16),
@@ -486,8 +539,16 @@
         ),
         name="hybrid",
     )(lq, lk, lv, decay.T, gain.reshape(heads, width), sq, sk, sv, lengths)
-    largest = jnp.finfo(bf16).max
-    return tuple(jnp.minimum(x, largest) for x in (light, soft))
+    whole = jax.ShapeDtypeStruct(lq.shape, bf16)
+    return pl.pallas_call(
+        finish,
+        out_shape=(whole, whole),
+        in_specs=[vmem] * 8,
+        out_specs=(anywhere, anywhere),
+        scratch_shapes=[pltpu.VMEM((toks, ends), bf16), dma((3,))],
+        compiler_params=pltpu.CompilerParams(vmem_limit_bytes=4000000),
+        name="finish",
+    )(*left)
 
 
 def solution(mesh):

time: 31.4 us -> 31 us (0.987)
  other arithmetic: 1.5 us -> 0 us
  Pallas kernels: 29.1 us -> 30.2 us
    min x1 -> x0, other arithmetic: 1.5 us -> none  [body(): return tuple((jnp.minimum(x, largest) for x in (light, soft)))]
    pallas_call x1 -> x2, Pallas kernels: 29.1 us -> 30.2 us  [the longest x1 28.8 us: body(): pl.pallas_call(functools.partial(kernel, n, width), out_shape=(out, out,...]
where the time goes in v4:
time: 31 us; the launch traced here: 30.8 us
  Pallas kernels  30.2 us (97%)
  between operations  0.64 us (2%)
    pallas_call x1, Pallas kernels, body(): pl.pallas_call(functools.partial(kernel, n, width), out_shape=(out, out,...  28.8 us
    pallas_call x1, Pallas kernels, body(): pl.pallas_call(finish, out_shape=(whole, whole), in_specs=[vmem] * 8, out...  1.33 us

profile of v4, /device:TPU:24, one launch (start us, length us, event | category | flops | bytes accessed | tf_op | source)
XLA Modules:
  0.0 30.8 jit_solution(10435089691632854109)
XLA Ops:
  0.6 28.8 %hybrid.1 = (bf16[256,2048]{1,0:T(8,128)(2,1)S(1)}, bf16[256,2048]{1,0:T(8,128)(2,1)S(1)}, bf16[256,256]{1,0:T(8,128)(2,1)S(1)}, bf16[2,128,128]{2,1,0:T(8,128)(...) custom-call(bf16[256,2048]{1,0:T(8,128)(2,1)} %lq_hbm.1, ...), custom_call_target="tpu_custom_call" | custom-call | tf_op jit(solution)/shard_map/hybrid/pallas_call | solution.py:511
  29.5 1.3 %finish.1 = (bf16[256,2048]{1,0:T(8,128)(2,1)}, bf16[256,2048]{1,0:T(8,128)(2,1)}) custom-call(bf16[256,2048]{1,0:T(8,128)(2,1)S(1)} %get-tuple-element.10.light, bf16[256,2048]{1,0:T(8,128)(2,1)S(1)} %get-tuple-element.11.soft, bf16[256,256]{1,0:T(8,128)(2,1)S(1)} %get-tuple-element.12.end_q, bf16[2,128,128]{2,1,0:T(8,128)(2,1)S(1)} %get-tuple-element.13.end_state, ...), custom_call_target="tpu_custom_call" | custom-call | tf_op jit(solution)/shard_map/finish/pallas_call | solution.py:543

commit v5 on v4

--- a/solution.py
+++ b/solution.py
@@ -51,6 +51,17 @@
     scale = width ** (-0.5)
     bf16, f32 = jnp.bfloat16, jnp.float32
 
+    barrier = pltpu.get_barrier_semaphore()
+
+    @pl.when(me > 0)
+    def _():
+        pl.semaphore_signal(barrier, inc=1, device_id={"seq": me - 1}, device_id_type=MESH)
+
+    if packed:
+        @pl.when(me == n - 2)
+        def _():
+            pl.semaphore_signal(barrier, inc=1, device_id=right, device_id_type=MESH)
+
     copies = [
         pltpu.make_async_copy(src, dst, local_sem.at[i])
         for i, (src, dst) in enumerate((
@@ -59,19 +70,8 @@
             (lengths_hbm, lengths),
         ))
     ]
-    for copy in copies:
+    for copy in (copies[0], copies[1], copies[2], copies[8]):
         copy.start()
-
-    barrier = pltpu.get_barrier_semaphore()
-
-    @pl.when(me > 0)
-    def _():
-        pl.semaphore_signal(barrier, inc=1, device_id={"seq": me - 1}, device_id_type=MESH)
-
-    if packed:
-        @pl.when(me == n - 2)
-        def _():
-            pl.semaphore_signal(barrier, inc=1, device_id=right, device_id_type=MESH)
 
     @pl.when(True if packed else me < n - 1)
     def _():
@@ -103,6 +103,11 @@
             device_id=right, device_id_type=MESH,
         )
 
+    front_copy = pltpu.make_async_remote_copy(
+        src_ref=kvbuf.at[0, :half], dst_ref=kvbuf.at[1, :half],
+        send_sem=kv_send.at[0, 0], recv_sem=kv_recv.at[1, 0],
+        device_id=right, device_id_type=MESH,
+    )
     query_copy = pltpu.make_async_remote_copy(
         src_ref=lq_hbm.at[:half], dst_ref=later_q, send_sem=q_send, recv_sem=q_recv,
         device_id={"seq": me - 1}, device_id_type=MESH,
@@ -119,15 +124,18 @@
     copies[0].wait()
     copies[1].wait()
 
-    @pl.when(me < last)
-    def _():
-        for p in range(PIECES // 2):
-            kv_copy(0, p).start()
+    if packed:
+        @pl.when(packs)
+        def _():
+            front_copy.start()
 
     @pl.when(forwards)
     def _():
-        for p in range(PIECES // 2, PIECES):
+        for p in range(PIECES):
             kv_copy(0, p).start()
+
+    for copy in copies[3:8]:
+        copy.start()
 
     copies[2].wait()
     copies[8].wait()
@@ -219,6 +227,12 @@
         each = PIECES // units
         for p in range(u * each, (u + 1) * each):
             needed = True if not packed else (me < last) | (step < last) | (p < PIECES // 2)
+            if packed and isinstance(step, int) and p < PIECES // 2:
+                needed = me < last
+                if p == 0:
+                    @pl.when(unpacks)
+                    def _():
+                        front_copy.wait_recv()
 
             @pl.when(needed)
             def _():
@@ -445,11 +459,17 @@
         def _():
             query_copy.wait_send()
 
+        @pl.when(packs)
+        def _():
+            front_copy.wait_send()
+
     @pl.when(me < n - 1)
     def _():
         def sent_blocks(step, carry):
             for p in range(PIECES):
-                sent = True if not packed else (me < n - 2) | (step < n - 2) | (p < PIECES // 2)
+                low = p < PIECES // 2
+                front = (step < n - 2) & ((step > 0) | (not low)) | (step == n - 2) & low
+                sent = True if not packed else (me < n - 2) | front
 
                 @pl.when(sent)
                 def _():

time: 31 us -> 31 us (level)
  no operation moved by 1% of the time
where the time goes in v5:
time: 31 us; the launch traced here: 30.8 us
  Pallas kernels  30.2 us (97%)
  between operations  0.64 us (2%)
    pallas_call x1, Pallas kernels, body(): pl.pallas_call(functools.partial(kernel, n, width), out_shape=(out, out,...  28.9 us
    pallas_call x1, Pallas kernels, body(): pl.pallas_call(finish, out_shape=(whole, whole), in_specs=[vmem] * 8, out...  1.33 us

profile of v5, /device:TPU:24, one launch (start us, length us, event | category | flops | bytes accessed | tf_op | source)
XLA Modules:
  0.0 30.8 jit_solution(13723954146865004597)
XLA Ops:
  0.6 28.9 %hybrid.1 = (bf16[256,2048]{1,0:T(8,128)(2,1)S(1)}, bf16[256,2048]{1,0:T(8,128)(2,1)S(1)}, bf16[256,256]{1,0:T(8,128)(2,1)S(1)}, bf16[2,128,128]{2,1,0:T(8,128)(...) custom-call(bf16[256,2048]{1,0:T(8,128)(2,1)} %lq_hbm.1, ...), custom_call_target="tpu_custom_call" | custom-call | tf_op jit(solution)/shard_map/hybrid/pallas_call | solution.py:531
  29.5 1.3 %finish.1 = (bf16[256,2048]{1,0:T(8,128)(2,1)}, bf16[256,2048]{1,0:T(8,128)(2,1)}) custom-call(bf16[256,2048]{1,0:T(8,128)(2,1)S(1)} %get-tuple-element.10.light, bf16[256,2048]{1,0:T(8,128)(2,1)S(1)} %get-tuple-element.11.soft, bf16[256,256]{1,0:T(8,128)(2,1)S(1)} %get-tuple-element.12.end_q, bf16[2,128,128]{2,1,0:T(8,128)(2,1)S(1)} %get-tuple-element.13.end_state, ...), custom_call_target="tpu_custom_call" | custom-call | tf_op jit(solution)/shard_map/finish/pallas_call | solution.py:563
